TPU v7x, 32 devices: a whole 2x2x4 slice. The times are simulated.
32 devices in a mesh: mkt: 4 (over z), prod: 2 (over core), draw: 4 (over y, x).
Axes of the slice: x: 2, y: 2, z: 4, core: 2. Of those that a mesh axis runs over, the one named last changes fastest.
Arguments:
- start_utility: float32 [1024, 256], P('mkt', 'prod'), may hold values from -5 to -2
- log_shares: float32 [1024, 256], P('mkt', 'prod'), may hold values from -9 to -5
- characteristics: float32 [1024, 8, 256], P('mkt', None, 'prod'), may hold values from -2.5 to 2.5
- coef_scale: float32 [8], replicated, may hold values from 0.1 to 0.3
- taste_draws: float32 [1024, 8, 2048], P('mkt', None, 'draw'), may hold values from -2.5 to 2.5
Outputs:
- mean_utility: float32 [1024, 256], P('mkt', 'prod')
- step_norms: float32 [2], replicated
All inputs are finite; a program needn't handle non-finite values.
Results may differ from a plain program's by a relative error of at most 0.0001.
Values sent between devices are 32-bit elements; how exact they have to be, the bound alone decides.
A program may use at most 64 MiB of HBM per device.

v0:
```python
import math
import jax
import jax.numpy as jnp
from jax import lax
from jax.sharding import PartitionSpec as P

R = 2048
ITERS = 2


def exponent(chars_part, scaled_part, util_part):
    spread = jnp.einsum("mkj,mkr->mjr", chars_part, scaled_part, precision=lax.Precision.HIGHEST)
    return jnp.exp(util_part[:, :, None] + spread)


def shards(start_utility, log_shares, characteristics, coef_scale, taste_draws):
    markets, coef_count, local_prod = characteristics.shape
    local_draws = taste_draws.shape[2]
    scaled = taste_draws * coef_scale[None, :, None]
    block_size = math.gcd(markets, 32)
    block_count = markets // block_size
    scaled_blocks = scaled.reshape(block_count, block_size, coef_count, local_draws)
    all_chars = lax.all_gather(characteristics, "prod", axis=2, tiled=True)
    all_blocks = all_chars.reshape(block_count, block_size, coef_count, -1)
    offset = lax.axis_index("prod") * local_prod
    utility = start_utility
    norm_list = []
    for iteration in range(ITERS):
        full_utility = lax.all_gather(utility, "prod", axis=1, tiled=True)

        def whole_pass(inputs):
            chars_part, scaled_part, util_part = inputs
            exp_util = exponent(chars_part, scaled_part, util_part)
            denominator = 1.0 + jnp.sum(exp_util, axis=1, keepdims=True)
            own_part = lax.dynamic_slice_in_dim(exp_util, offset, local_prod, 1)
            return jnp.sum(own_part / denominator, axis=2)

        summed = lax.map(
            whole_pass,
            (all_blocks, scaled_blocks, full_utility.reshape(block_count, block_size, -1)),
        )
        predicted = lax.psum(summed.reshape(markets, local_prod), "draw") / R
        updated = utility + log_shares - jnp.log(predicted)
        change = updated - utility
        square_sum = jnp.sum(change * change)
        norm_list.append(lax.psum(square_sum, ("mkt", "prod")))
        utility = updated
    totals = jnp.stack(norm_list)
    cell_count = markets * local_prod * lax.axis_size("mkt") * lax.axis_size("prod")
    step_norms = jnp.sqrt(totals / cell_count + 1e-06)
    return (utility, step_norms)


def solution(mesh):
    return jax.shard_map(
        shards,
        mesh=mesh,
        in_specs=(
            P("mkt", "prod"),
            P("mkt", "prod"),
            P("mkt", None, "prod"),
            P(),
            P("mkt", None, "draw"),
        ),
        out_specs=(P("mkt", "prod"), P()),
        check_vma=False,
    )
```

profile of v0, /device:TPU:0, one launch (start us, length us, event | category | flops | bytes accessed | tf_op | source)
XLA Modules:
  0.0 413.3 jit_solution(8134202163170635806)
XLA Ops:
  7.2 0.7 all-gather.2.cloned.1.call-update
  7.9 2.3 all_gather.9
  10.3 4.7 %broadcast_multiply_fusion = f32[256,8,512]{2,1,0:T(8,128)} fusion(f32[256,8,512]{2,1,0:T(8,128)} %param.13, f32[8]{0:T(128)} %param.12), kind=kLoop, calls=%fused_computation.22 | loop fusion | flops 1048576 | bytes 8388640 | tf_op jit(solution)/shard_map/mul | solution.py:19
  15.0 7.4 %all-gather.2.cloned.1.call-done = f32[256,8,256]{2,1,0:T(8,128)} async-done(((f32[256,8,128]{2,1,0:T(8,128)}), f32[256,8,256]{2,1,0:T(8,128)}) %all-gather.2.cloned.1.call-update) | async-done | bytes 2097168 | tf_op jit(solution)/shard_map/all_gather | solution.py:23
  22.4 136.7 %while.24 = (s32[]{:T(128)}, f32[8,32,128]{2,1,0:T(8,128)S(1)}, f32[8,32,256]{2,1,0:T(8,128)S(1)}, f32[8,32,8,256]{3,2,1,0:T(8,128)}, f32[8,32,8,512]{3,2,1,0:T(8,128)}, /*index=5*/s32[]{:T(128)}, s32[]{:T(128)}) while((s32[]{:T(128)}, f32[8,32,128]{2,1,0:T(8,128)S(1)}, f32[8,32,256]{2,1,0:T(8,128)S(1)}, f32[8,32,8,256]{3,2,1,0:T(8,128)}, ...), condition=%wide.region_3.4_spmd, body=%wide.region_0.3_spmd.sunk | while | flops 415232000 | bytes 26362968 | solution.py:38
  22.4 16.4 %fusion.20 = (f32[32,512]{1,0:T(8,128)S(1)}, f32[32,256,512]{2,1,0:T(8,128)S(1)}) fusion(f32[8,32,8,512]{3,2,1,0:T(8,128)} %get-tuple-element.285, s32[]{:T(128)} %get-tuple-element.274, f32[8,32,8,256]{3,2,1,0:T(8,128)} %get-tuple-element.284, f32[32,256]{1,0:T(8,128)S(1)} %dynamic-slice_bitcast_fusion.4), kind=kOutput, calls=%fused_computation.30.clone.1 | convolution fusion | flops 411025408 | bytes 17662976 | tf_op jit(solution)/shard_map/while/body/eval_jaxpr/mkj,mkr->mjr/dot_general | solution.py:12
  38.9 0.7 fusion.21
  39.6 16.3 %fusion.20 = (f32[32,512]{1,0:T(8,128)S(1)}, f32[32,256,512]{2,1,0:T(8,128)S(1)}) fusion(f32[8,32,8,512]{3,2,1,0:T(8,128)} %get-tuple-element.285, s32[]{:T(128)} %get-tuple-element.274, f32[8,32,8,256]{3,2,1,0:T(8,128)} %get-tuple-element.284, f32[32,256]{1,0:T(8,128)S(1)} %dynamic-slice_bitcast_fusion.4), kind=kOutput, calls=%fused_computation.30.clone.1 | convolution fusion | flops 411025408 | bytes 17662976 | tf_op jit(solution)/shard_map/while/body/eval_jaxpr/mkj,mkr->mjr/dot_general | solution.py:12
  56.7 16.3 %fusion.20 = (f32[32,512]{1,0:T(8,128)S(1)}, f32[32,256,512]{2,1,0:T(8,128)S(1)}) fusion(f32[8,32,8,512]{3,2,1,0:T(8,128)} %get-tuple-element.285, s32[]{:T(128)} %get-tuple-element.274, f32[8,32,8,256]{3,2,1,0:T(8,128)} %get-tuple-element.284, f32[32,256]{1,0:T(8,128)S(1)} %dynamic-slice_bitcast_fusion.4), kind=kOutput, calls=%fused_computation.30.clone.1 | convolution fusion | flops 411025408 | bytes 17662976 | tf_op jit(solution)/shard_map/while/body/eval_jaxpr/mkj,mkr->mjr/dot_general | solution.py:12
  73.7 16.3 %fusion.20 = (f32[32,512]{1,0:T(8,128)S(1)}, f32[32,256,512]{2,1,0:T(8,128)S(1)}) fusion(f32[8,32,8,512]{3,2,1,0:T(8,128)} %get-tuple-element.285, s32[]{:T(128)} %get-tuple-element.274, f32[8,32,8,256]{3,2,1,0:T(8,128)} %get-tuple-element.284, f32[32,256]{1,0:T(8,128)S(1)} %dynamic-slice_bitcast_fusion.4), kind=kOutput, calls=%fused_computation.30.clone.1 | convolution fusion | flops 411025408 | bytes 17662976 | tf_op jit(solution)/shard_map/while/body/eval_jaxpr/mkj,mkr->mjr/dot_general | solution.py:12
  90.1 0.7 fusion.21
  90.8 16.3 %fusion.20 = (f32[32,512]{1,0:T(8,128)S(1)}, f32[32,256,512]{2,1,0:T(8,128)S(1)}) fusion(f32[8,32,8,512]{3,2,1,0:T(8,128)} %get-tuple-element.285, s32[]{:T(128)} %get-tuple-element.274, f32[8,32,8,256]{3,2,1,0:T(8,128)} %get-tuple-element.284, f32[32,256]{1,0:T(8,128)S(1)} %dynamic-slice_bitcast_fusion.4), kind=kOutput, calls=%fused_computation.30.clone.1 | convolution fusion | flops 411025408 | bytes 17662976 | tf_op jit(solution)/shard_map/while/body/eval_jaxpr/mkj,mkr->mjr/dot_general | solution.py:12
  107.9 16.3 %fusion.20 = (f32[32,512]{1,0:T(8,128)S(1)}, f32[32,256,512]{2,1,0:T(8,128)S(1)}) fusion(f32[8,32,8,512]{3,2,1,0:T(8,128)} %get-tuple-element.285, s32[]{:T(128)} %get-tuple-element.274, f32[8,32,8,256]{3,2,1,0:T(8,128)} %get-tuple-element.284, f32[32,256]{1,0:T(8,128)S(1)} %dynamic-slice_bitcast_fusion.4), kind=kOutput, calls=%fused_computation.30.clone.1 | convolution fusion | flops 411025408 | bytes 17662976 | tf_op jit(solution)/shard_map/while/body/eval_jaxpr/mkj,mkr->mjr/dot_general | solution.py:12
  125.0 16.3 %fusion.20 = (f32[32,512]{1,0:T(8,128)S(1)}, f32[32,256,512]{2,1,0:T(8,128)S(1)}) fusion(f32[8,32,8,512]{3,2,1,0:T(8,128)} %get-tuple-element.285, s32[]{:T(128)} %get-tuple-element.274, f32[8,32,8,256]{3,2,1,0:T(8,128)} %get-tuple-element.284, f32[32,256]{1,0:T(8,128)S(1)} %dynamic-slice_bitcast_fusion.4), kind=kOutput, calls=%fused_computation.30.clone.1 | convolution fusion | flops 411025408 | bytes 17662976 | tf_op jit(solution)/shard_map/while/body/eval_jaxpr/mkj,mkr->mjr/dot_general | solution.py:12
  142.0 16.3 %fusion.20 = (f32[32,512]{1,0:T(8,128)S(1)}, f32[32,256,512]{2,1,0:T(8,128)S(1)}) fusion(f32[8,32,8,512]{3,2,1,0:T(8,128)} %get-tuple-element.285, s32[]{:T(128)} %get-tuple-element.274, f32[8,32,8,256]{3,2,1,0:T(8,128)} %get-tuple-element.284, f32[32,256]{1,0:T(8,128)S(1)} %dynamic-slice_bitcast_fusion.4), kind=kOutput, calls=%fused_computation.30.clone.1 | convolution fusion | flops 411025408 | bytes 17662976 | tf_op jit(solution)/shard_map/while/body/eval_jaxpr/mkj,mkr->mjr/dot_general | solution.py:12
  159.8 43.5 %all-reduce.4.cloned.1.call-done = f32[256,128]{1,0:T(8,128)} async-done(((f32[256,128]{1,0:T(8,128)}), f32[256,128]{1,0:T(8,128)}) %all-reduce.4.cloned.1.call-update) | async-done | bytes 131088 | tf_op jit(solution)/shard_map/psum | solution.py:42
  203.4 0.9 log_subtract_fusion.1
  204.3 2.0 all_gather.11
  206.3 136.8 %while.25 = (s32[]{:T(128)}, f32[8,32,128]{2,1,0:T(8,128)S(1)}, f32[8,32,256]{2,1,0:T(8,128)S(1)}, f32[8,32,8,256]{3,2,1,0:T(8,128)}, f32[8,32,8,512]{3,2,1,0:T(8,128)}, /*index=5*/s32[]{:T(128)}, s32[]{:T(128)}) while((s32[]{:T(128)}, f32[8,32,128]{2,1,0:T(8,128)S(1)}, f32[8,32,256]{2,1,0:T(8,128)S(1)}, f32[8,32,8,256]{3,2,1,0:T(8,128)}, ...), condition=%wide.region_8.9_spmd, body=%wide.region_5.8_spmd.sunk | while | flops 415232000 | bytes 26362968 | solution.py:38
  206.5 16.3 %fusion.22 = (f32[32,512]{1,0:T(8,128)S(1)}, f32[32,256,512]{2,1,0:T(8,128)S(1)}) fusion(f32[8,32,8,512]{3,2,1,0:T(8,128)} %get-tuple-element.306, s32[]{:T(128)} %get-tuple-element.295, f32[8,32,8,256]{3,2,1,0:T(8,128)} %get-tuple-element.305, f32[32,256]{1,0:T(8,128)S(1)} %dynamic-slice_bitcast_fusion.5), kind=kOutput, calls=%fused_computation.31.clone.1 | convolution fusion | flops 411025408 | bytes 17662976 | tf_op jit(solution)/shard_map/while/body/eval_jaxpr/mkj,mkr->mjr/dot_general | solution.py:12
  223.6 16.3 %fusion.22 = (f32[32,512]{1,0:T(8,128)S(1)}, f32[32,256,512]{2,1,0:T(8,128)S(1)}) fusion(f32[8,32,8,512]{3,2,1,0:T(8,128)} %get-tuple-element.306, s32[]{:T(128)} %get-tuple-element.295, f32[8,32,8,256]{3,2,1,0:T(8,128)} %get-tuple-element.305, f32[32,256]{1,0:T(8,128)S(1)} %dynamic-slice_bitcast_fusion.5), kind=kOutput, calls=%fused_computation.31.clone.1 | convolution fusion | flops 411025408 | bytes 17662976 | tf_op jit(solution)/shard_map/while/body/eval_jaxpr/mkj,mkr->mjr/dot_general | solution.py:12
  240.7 16.3 %fusion.22 = (f32[32,512]{1,0:T(8,128)S(1)}, f32[32,256,512]{2,1,0:T(8,128)S(1)}) fusion(f32[8,32,8,512]{3,2,1,0:T(8,128)} %get-tuple-element.306, s32[]{:T(128)} %get-tuple-element.295, f32[8,32,8,256]{3,2,1,0:T(8,128)} %get-tuple-element.305, f32[32,256]{1,0:T(8,128)S(1)} %dynamic-slice_bitcast_fusion.5), kind=kOutput, calls=%fused_computation.31.clone.1 | convolution fusion | flops 411025408 | bytes 17662976 | tf_op jit(solution)/shard_map/while/body/eval_jaxpr/mkj,mkr->mjr/dot_general | solution.py:12
  257.7 16.3 %fusion.22 = (f32[32,512]{1,0:T(8,128)S(1)}, f32[32,256,512]{2,1,0:T(8,128)S(1)}) fusion(f32[8,32,8,512]{3,2,1,0:T(8,128)} %get-tuple-element.306, s32[]{:T(128)} %get-tuple-element.295, f32[8,32,8,256]{3,2,1,0:T(8,128)} %get-tuple-element.305, f32[32,256]{1,0:T(8,128)S(1)} %dynamic-slice_bitcast_fusion.5), kind=kOutput, calls=%fused_computation.31.clone.1 | convolution fusion | flops 411025408 | bytes 17662976 | tf_op jit(solution)/shard_map/while/body/eval_jaxpr/mkj,mkr->mjr/dot_general | solution.py:12
  274.8 16.3 %fusion.22 = (f32[32,512]{1,0:T(8,128)S(1)}, f32[32,256,512]{2,1,0:T(8,128)S(1)}) fusion(f32[8,32,8,512]{3,2,1,0:T(8,128)} %get-tuple-element.306, s32[]{:T(128)} %get-tuple-element.295, f32[8,32,8,256]{3,2,1,0:T(8,128)} %get-tuple-element.305, f32[32,256]{1,0:T(8,128)S(1)} %dynamic-slice_bitcast_fusion.5), kind=kOutput, calls=%fused_computation.31.clone.1 | convolution fusion | flops 411025408 | bytes 17662976 | tf_op jit(solution)/shard_map/while/body/eval_jaxpr/mkj,mkr->mjr/dot_general | solution.py:12
  291.9 16.3 %fusion.22 = (f32[32,512]{1,0:T(8,128)S(1)}, f32[32,256,512]{2,1,0:T(8,128)S(1)}) fusion(f32[8,32,8,512]{3,2,1,0:T(8,128)} %get-tuple-element.306, s32[]{:T(128)} %get-tuple-element.295, f32[8,32,8,256]{3,2,1,0:T(8,128)} %get-tuple-element.305, f32[32,256]{1,0:T(8,128)S(1)} %dynamic-slice_bitcast_fusion.5), kind=kOutput, calls=%fused_computation.31.clone.1 | convolution fusion | flops 411025408 | bytes 17662976 | tf_op jit(solution)/shard_map/while/body/eval_jaxpr/mkj,mkr->mjr/dot_general | solution.py:12
  309.0 16.3 %fusion.22 = (f32[32,512]{1,0:T(8,128)S(1)}, f32[32,256,512]{2,1,0:T(8,128)S(1)}) fusion(f32[8,32,8,512]{3,2,1,0:T(8,128)} %get-tuple-element.306, s32[]{:T(128)} %get-tuple-element.295, f32[8,32,8,256]{3,2,1,0:T(8,128)} %get-tuple-element.305, f32[32,256]{1,0:T(8,128)S(1)} %dynamic-slice_bitcast_fusion.5), kind=kOutput, calls=%fused_computation.31.clone.1 | convolution fusion | flops 411025408 | bytes 17662976 | tf_op jit(solution)/shard_map/while/body/eval_jaxpr/mkj,mkr->mjr/dot_general | solution.py:12
  326.1 16.3 %fusion.22 = (f32[32,512]{1,0:T(8,128)S(1)}, f32[32,256,512]{2,1,0:T(8,128)S(1)}) fusion(f32[8,32,8,512]{3,2,1,0:T(8,128)} %get-tuple-element.306, s32[]{:T(128)} %get-tuple-element.295, f32[8,32,8,256]{3,2,1,0:T(8,128)} %get-tuple-element.305, f32[32,256]{1,0:T(8,128)S(1)} %dynamic-slice_bitcast_fusion.5), kind=kOutput, calls=%fused_computation.31.clone.1 | convolution fusion | flops 411025408 | bytes 17662976 | tf_op jit(solution)/shard_map/while/body/eval_jaxpr/mkj,mkr->mjr/dot_general | solution.py:12
  342.4 0.7 fusion.23
  343.8 42.4 %all-reduce.6.cloned.1.call-done = f32[256,128]{1,0:T(8,128)} async-done(((f32[256,128]{1,0:T(8,128)}), f32[256,128]{1,0:T(8,128)}) %all-reduce.6.cloned.1.call-update) | async-done | bytes 131088 | tf_op jit(solution)/shard_map/psum | solution.py:42
  386.2 2.2 multiply_reduce_fusion.1
  388.4 16.6 %all-reduce = (f32[1]{0:T(128)}, f32[1]{0:T(128)}) all-reduce(f32[1]{0:T(128)} %bitcast.15, f32[1]{0:T(128)} %bitcast.14), channel_id=1, replica_groups=mesh['mkt'=4,'prod'=2,'draw'=4] {'mkt','prod'}, use_global_device_ids=true, to_apply=%region_13.14 | all-reduce | flops 2 | bytes 16 | tf_op jit(solution)/shard_map/psum | solution.py:46
  405.0 1.8 fusion.13
  (76 shorter events, 10.6 us)
Async XLA Ops:
  7.2 15.2 %all-gather.2.cloned.1.call-start = ((), (), s32[]{:S(2)}) async-start(), calls=%async_computation | async-start | bytes 3145728 | tf_op jit(solution)/shard_map/all_gather | solution.py:23
  7.9 195.5 %all-reduce.4.cloned.1.call-start = ((), (), s32[]{:S(2)}) async-start(), calls=%async_computation.1 | async-start | bytes 262144 | tf_op jit(solution)/shard_map/psum | solution.py:42
  22.4 181.0 %copy-start = (f32[256,128]{1,0:T(8,128)S(1)}, f32[256,128]{1,0:T(8,128)}, u32[]{:S(2)}) copy-start(f32[256,128]{1,0:T(8,128)} %param.9) | copy-start | bytes 393220
  22.4 181.0 %copy-start.1 = (f32[256,128]{1,0:T(8,128)S(1)}, f32[256,128]{1,0:T(8,128)}, u32[]{:S(2)}) copy-start(f32[256,128]{1,0:T(8,128)} %param.10) | copy-start | bytes 393220
  159.1 0.7 copy-start.3
  159.8 226.4 %all-reduce.6.cloned.1.call-start = ((), (), s32[]{:S(2)}) async-start(), calls=%async_computation.2 | async-start | bytes 262144 | tf_op jit(solution)/shard_map/psum | solution.py:42
  343.1 0.7 copy-start.2
Sparse Core Ops, SparseCore 0:
  9.5 12.8 all-gather.1
  159.9 43.4 all-reduce.3
  343.9 42.1 all-reduce.5
where the time goes:
time: 414 us; the launch traced here: 413 us
  matrix products  261 us (63%)
  waiting for transfers between devices  94 us (23%)
  blocking collectives  20.9 us (5%)
  other arithmetic  20.5 us (5%)
  between operations  13.8 us (3%)
    dot_general x16, matrix products, exponent(): jnp.einsum('mkj,mkr->mjr', chars_part, scaled_part, precision=lax.Precisi...  261 us
    psum x2, waiting for transfers between devices, shards(): predicted = lax.psum(summed.reshape(markets, local_prod), 'draw') / R  85.9 us
    psum x1, blocking collectives, shards(): norm_list.append(lax.psum(square_sum, ('mkt', 'prod')))  16.6 us
    reduce_sum x16, other arithmetic, whole_pass(): return jnp.sum(own_part / denominator, axis=2)  10.7 us
  transfers between devices with their start and end apart: 3, of which 3 were waited for; matrix products, arithmetic and copies ran while one was open for 1% of the time, Pallas kernels for 0%

commit v1 on v0

--- a/solution.py
+++ b/solution.py
@@ -39,7 +39,7 @@
             whole_pass,
             (all_blocks, scaled_blocks, full_utility.reshape(block_count, block_size, -1)),
         )
-        predicted = lax.psum(summed.reshape(markets, local_prod), "draw") / R
+        predicted = jnp.sum(lax.all_gather(summed.reshape(markets, local_prod), "draw"), axis=0) / R
         updated = utility + log_shares - jnp.log(predicted)
         change = updated - utility
         square_sum = jnp.sum(change * change)

time: 414 us -> 344 us (0.83)
  waiting for transfers between devices: 94 us -> 8.12 us
  blocking collectives: 20.9 us -> 39.9 us
    psum x2 -> x0, waiting for transfers between devices: 85.9 us -> none  [shards(): predicted = lax.psum(summed.reshape(markets, local_prod), 'draw') / R]
    all_gather x0 -> x2, blocking collectives: none -> 20.3 us  [shards(): lax.all_gather(summed.reshape(markets, local_prod), 'draw')]
  transfers between devices with their start and end apart: 3 -> 1, of which waited for: 3 -> 1; matrix products, arithmetic and copies ran while one was open for 1% -> 1% of each run, Pallas kernels for 0% -> 0%
where the time goes in v1:
time: 344 us
  matrix products  261 us (76%)
  blocking collectives  39.9 us (12%)
  other arithmetic  18.7 us (5%)
  between operations  14.1 us (4%)
  waiting for transfers between devices  8.12 us (2%)
    dot_general x16, matrix products, exponent(): jnp.einsum('mkj,mkr->mjr', chars_part, scaled_part, precision=lax.Precisi...  261 us
    all_gather x2, blocking collectives, shards(): lax.all_gather(summed.reshape(markets, local_prod), 'draw')  20.3 us
    psum x1, blocking collectives, shards(): norm_list.append(lax.psum(square_sum, ('mkt', 'prod')))  15.3 us
    reduce_sum x16, other arithmetic, whole_pass(): return jnp.sum(own_part / denominator, axis=2)  10.7 us
    all_gather x1, waiting for transfers between devices, shards(): all_chars = lax.all_gather(characteristics, 'prod', axis=2, tiled=True)  7.44 us
  transfers between devices with their start and end apart: 1, of which 1 were waited for; matrix products, arithmetic and copies ran while one was open for 1% of the time, Pallas kernels for 0%

profile of v1, /device:TPU:0, one launch (start us, length us, event | category | flops | bytes accessed | tf_op | source)
XLA Modules:
  0.0 343.6 jit_solution(14407108026044058613)
XLA Ops:
  7.2 0.7 all-gather.2.cloned.1.call-update
  7.9 2.3 all_gather.15
  10.2 4.7 %broadcast_multiply_fusion = f32[256,8,512]{2,1,0:T(8,128)} fusion(f32[256,8,512]{2,1,0:T(8,128)} %param.13, f32[8]{0:T(128)} %param.12), kind=kLoop, calls=%fused_computation.22 | loop fusion | flops 1048576 | bytes 8388640 | tf_op jit(solution)/shard_map/mul | solution.py:19
  14.9 7.4 %all-gather.2.cloned.1.call-done = f32[256,8,256]{2,1,0:T(8,128)} async-done(((f32[256,8,128]{2,1,0:T(8,128)}), f32[256,8,256]{2,1,0:T(8,128)}) %all-gather.2.cloned.1.call-update) | async-done | bytes 2097168 | tf_op jit(solution)/shard_map/all_gather | solution.py:23
  22.4 136.7 %while.24 = (s32[]{:T(128)}, f32[8,32,128]{2,1,0:T(8,128)S(1)}, f32[8,32,256]{2,1,0:T(8,128)S(1)}, f32[8,32,8,256]{3,2,1,0:T(8,128)}, f32[8,32,8,512]{3,2,1,0:T(8,128)}, /*index=5*/s32[]{:T(128)}, s32[]{:T(128)}) while((s32[]{:T(128)}, f32[8,32,128]{2,1,0:T(8,128)S(1)}, f32[8,32,256]{2,1,0:T(8,128)S(1)}, f32[8,32,8,256]{3,2,1,0:T(8,128)}, ...), condition=%wide.region_3.4_spmd, body=%wide.region_0.3_spmd.sunk | while | flops 415232000 | bytes 26362968 | solution.py:38
  22.4 16.4 %fusion.20 = (f32[32,512]{1,0:T(8,128)S(1)}, f32[32,256,512]{2,1,0:T(8,128)S(1)}) fusion(f32[8,32,8,512]{3,2,1,0:T(8,128)} %get-tuple-element.285, s32[]{:T(128)} %get-tuple-element.274, f32[8,32,8,256]{3,2,1,0:T(8,128)} %get-tuple-element.284, f32[32,256]{1,0:T(8,128)S(1)} %dynamic-slice_bitcast_fusion.4), kind=kOutput, calls=%fused_computation.30.clone.1 | convolution fusion | flops 411025408 | bytes 17662976 | tf_op jit(solution)/shard_map/while/body/eval_jaxpr/mkj,mkr->mjr/dot_general | solution.py:12
  38.9 0.7 fusion.21
  39.6 16.3 %fusion.20 = (f32[32,512]{1,0:T(8,128)S(1)}, f32[32,256,512]{2,1,0:T(8,128)S(1)}) fusion(f32[8,32,8,512]{3,2,1,0:T(8,128)} %get-tuple-element.285, s32[]{:T(128)} %get-tuple-element.274, f32[8,32,8,256]{3,2,1,0:T(8,128)} %get-tuple-element.284, f32[32,256]{1,0:T(8,128)S(1)} %dynamic-slice_bitcast_fusion.4), kind=kOutput, calls=%fused_computation.30.clone.1 | convolution fusion | flops 411025408 | bytes 17662976 | tf_op jit(solution)/shard_map/while/body/eval_jaxpr/mkj,mkr->mjr/dot_general | solution.py:12
  55.9 0.7 fusion.21
  56.7 16.3 %fusion.20 = (f32[32,512]{1,0:T(8,128)S(1)}, f32[32,256,512]{2,1,0:T(8,128)S(1)}) fusion(f32[8,32,8,512]{3,2,1,0:T(8,128)} %get-tuple-element.285, s32[]{:T(128)} %get-tuple-element.274, f32[8,32,8,256]{3,2,1,0:T(8,128)} %get-tuple-element.284, f32[32,256]{1,0:T(8,128)S(1)} %dynamic-slice_bitcast_fusion.4), kind=kOutput, calls=%fused_computation.30.clone.1 | convolution fusion | flops 411025408 | bytes 17662976 | tf_op jit(solution)/shard_map/while/body/eval_jaxpr/mkj,mkr->mjr/dot_general | solution.py:12
  73.7 16.3 %fusion.20 = (f32[32,512]{1,0:T(8,128)S(1)}, f32[32,256,512]{2,1,0:T(8,128)S(1)}) fusion(f32[8,32,8,512]{3,2,1,0:T(8,128)} %get-tuple-element.285, s32[]{:T(128)} %get-tuple-element.274, f32[8,32,8,256]{3,2,1,0:T(8,128)} %get-tuple-element.284, f32[32,256]{1,0:T(8,128)S(1)} %dynamic-slice_bitcast_fusion.4), kind=kOutput, calls=%fused_computation.30.clone.1 | convolution fusion | flops 411025408 | bytes 17662976 | tf_op jit(solution)/shard_map/while/body/eval_jaxpr/mkj,mkr->mjr/dot_general | solution.py:12
  90.1 0.7 fusion.21
  90.8 16.3 %fusion.20 = (f32[32,512]{1,0:T(8,128)S(1)}, f32[32,256,512]{2,1,0:T(8,128)S(1)}) fusion(f32[8,32,8,512]{3,2,1,0:T(8,128)} %get-tuple-element.285, s32[]{:T(128)} %get-tuple-element.274, f32[8,32,8,256]{3,2,1,0:T(8,128)} %get-tuple-element.284, f32[32,256]{1,0:T(8,128)S(1)} %dynamic-slice_bitcast_fusion.4), kind=kOutput, calls=%fused_computation.30.clone.1 | convolution fusion | flops 411025408 | bytes 17662976 | tf_op jit(solution)/shard_map/while/body/eval_jaxpr/mkj,mkr->mjr/dot_general | solution.py:12
  107.9 16.3 %fusion.20 = (f32[32,512]{1,0:T(8,128)S(1)}, f32[32,256,512]{2,1,0:T(8,128)S(1)}) fusion(f32[8,32,8,512]{3,2,1,0:T(8,128)} %get-tuple-element.285, s32[]{:T(128)} %get-tuple-element.274, f32[8,32,8,256]{3,2,1,0:T(8,128)} %get-tuple-element.284, f32[32,256]{1,0:T(8,128)S(1)} %dynamic-slice_bitcast_fusion.4), kind=kOutput, calls=%fused_computation.30.clone.1 | convolution fusion | flops 411025408 | bytes 17662976 | tf_op jit(solution)/shard_map/while/body/eval_jaxpr/mkj,mkr->mjr/dot_general | solution.py:12
  125.0 16.3 %fusion.20 = (f32[32,512]{1,0:T(8,128)S(1)}, f32[32,256,512]{2,1,0:T(8,128)S(1)}) fusion(f32[8,32,8,512]{3,2,1,0:T(8,128)} %get-tuple-element.285, s32[]{:T(128)} %get-tuple-element.274, f32[8,32,8,256]{3,2,1,0:T(8,128)} %get-tuple-element.284, f32[32,256]{1,0:T(8,128)S(1)} %dynamic-slice_bitcast_fusion.4), kind=kOutput, calls=%fused_computation.30.clone.1 | convolution fusion | flops 411025408 | bytes 17662976 | tf_op jit(solution)/shard_map/while/body/eval_jaxpr/mkj,mkr->mjr/dot_general | solution.py:12
  142.0 16.3 %fusion.20 = (f32[32,512]{1,0:T(8,128)S(1)}, f32[32,256,512]{2,1,0:T(8,128)S(1)}) fusion(f32[8,32,8,512]{3,2,1,0:T(8,128)} %get-tuple-element.285, s32[]{:T(128)} %get-tuple-element.274, f32[8,32,8,256]{3,2,1,0:T(8,128)} %get-tuple-element.284, f32[32,256]{1,0:T(8,128)S(1)} %dynamic-slice_bitcast_fusion.4), kind=kOutput, calls=%fused_computation.30.clone.1 | convolution fusion | flops 411025408 | bytes 17662976 | tf_op jit(solution)/shard_map/while/body/eval_jaxpr/mkj,mkr->mjr/dot_general | solution.py:12
  159.1 10.3 %all_gather.17 = f32[4,256,128]{2,1,0:T(8,128)S(1)} all-gather(f32[1,256,128]{2,1,0:T(8,128)S(1)} %bitcast.56), channel_id=1, replica_groups=mesh['mkt'=4,'prod'=2,'draw'=4] {'draw'}, dimensions={0}, use_global_device_ids=true | all-gather | bytes 655360 | tf_op jit(solution)/shard_map/all_gather | solution.py:42
  169.5 2.0 all_gather.18
  171.5 136.8 %while.25 = (s32[]{:T(128)}, f32[8,32,128]{2,1,0:T(8,128)S(1)}, f32[8,32,256]{2,1,0:T(8,128)S(1)}, f32[8,32,8,256]{3,2,1,0:T(8,128)}, f32[8,32,8,512]{3,2,1,0:T(8,128)}, /*index=5*/s32[]{:T(128)}, s32[]{:T(128)}) while((s32[]{:T(128)}, f32[8,32,128]{2,1,0:T(8,128)S(1)}, f32[8,32,256]{2,1,0:T(8,128)S(1)}, f32[8,32,8,256]{3,2,1,0:T(8,128)}, ...), condition=%wide.region_8.9_spmd, body=%wide.region_5.8_spmd.sunk | while | flops 415232000 | bytes 26362968 | solution.py:38
  171.7 16.3 %fusion.22 = (f32[32,512]{1,0:T(8,128)S(1)}, f32[32,256,512]{2,1,0:T(8,128)S(1)}) fusion(f32[8,32,8,512]{3,2,1,0:T(8,128)} %get-tuple-element.306, s32[]{:T(128)} %get-tuple-element.295, f32[8,32,8,256]{3,2,1,0:T(8,128)} %get-tuple-element.305, f32[32,256]{1,0:T(8,128)S(1)} %dynamic-slice_bitcast_fusion.5), kind=kOutput, calls=%fused_computation.31.clone.1 | convolution fusion | flops 411025408 | bytes 17662976 | tf_op jit(solution)/shard_map/while/body/eval_jaxpr/mkj,mkr->mjr/dot_general | solution.py:12
  188.8 16.3 %fusion.22 = (f32[32,512]{1,0:T(8,128)S(1)}, f32[32,256,512]{2,1,0:T(8,128)S(1)}) fusion(f32[8,32,8,512]{3,2,1,0:T(8,128)} %get-tuple-element.306, s32[]{:T(128)} %get-tuple-element.295, f32[8,32,8,256]{3,2,1,0:T(8,128)} %get-tuple-element.305, f32[32,256]{1,0:T(8,128)S(1)} %dynamic-slice_bitcast_fusion.5), kind=kOutput, calls=%fused_computation.31.clone.1 | convolution fusion | flops 411025408 | bytes 17662976 | tf_op jit(solution)/shard_map/while/body/eval_jaxpr/mkj,mkr->mjr/dot_general | solution.py:12
  205.9 16.3 %fusion.22 = (f32[32,512]{1,0:T(8,128)S(1)}, f32[32,256,512]{2,1,0:T(8,128)S(1)}) fusion(f32[8,32,8,512]{3,2,1,0:T(8,128)} %get-tuple-element.306, s32[]{:T(128)} %get-tuple-element.295, f32[8,32,8,256]{3,2,1,0:T(8,128)} %get-tuple-element.305, f32[32,256]{1,0:T(8,128)S(1)} %dynamic-slice_bitcast_fusion.5), kind=kOutput, calls=%fused_computation.31.clone.1 | convolution fusion | flops 411025408 | bytes 17662976 | tf_op jit(solution)/shard_map/while/body/eval_jaxpr/mkj,mkr->mjr/dot_general | solution.py:12
  222.9 16.3 %fusion.22 = (f32[32,512]{1,0:T(8,128)S(1)}, f32[32,256,512]{2,1,0:T(8,128)S(1)}) fusion(f32[8,32,8,512]{3,2,1,0:T(8,128)} %get-tuple-element.306, s32[]{:T(128)} %get-tuple-element.295, f32[8,32,8,256]{3,2,1,0:T(8,128)} %get-tuple-element.305, f32[32,256]{1,0:T(8,128)S(1)} %dynamic-slice_bitcast_fusion.5), kind=kOutput, calls=%fused_computation.31.clone.1 | convolution fusion | flops 411025408 | bytes 17662976 | tf_op jit(solution)/shard_map/while/body/eval_jaxpr/mkj,mkr->mjr/dot_general | solution.py:12
  240.0 16.3 %fusion.22 = (f32[32,512]{1,0:T(8,128)S(1)}, f32[32,256,512]{2,1,0:T(8,128)S(1)}) fusion(f32[8,32,8,512]{3,2,1,0:T(8,128)} %get-tuple-element.306, s32[]{:T(128)} %get-tuple-element.295, f32[8,32,8,256]{3,2,1,0:T(8,128)} %get-tuple-element.305, f32[32,256]{1,0:T(8,128)S(1)} %dynamic-slice_bitcast_fusion.5), kind=kOutput, calls=%fused_computation.31.clone.1 | convolution fusion | flops 411025408 | bytes 17662976 | tf_op jit(solution)/shard_map/while/body/eval_jaxpr/mkj,mkr->mjr/dot_general | solution.py:12
  257.1 16.3 %fusion.22 = (f32[32,512]{1,0:T(8,128)S(1)}, f32[32,256,512]{2,1,0:T(8,128)S(1)}) fusion(f32[8,32,8,512]{3,2,1,0:T(8,128)} %get-tuple-element.306, s32[]{:T(128)} %get-tuple-element.295, f32[8,32,8,256]{3,2,1,0:T(8,128)} %get-tuple-element.305, f32[32,256]{1,0:T(8,128)S(1)} %dynamic-slice_bitcast_fusion.5), kind=kOutput, calls=%fused_computation.31.clone.1 | convolution fusion | flops 411025408 | bytes 17662976 | tf_op jit(solution)/shard_map/while/body/eval_jaxpr/mkj,mkr->mjr/dot_general | solution.py:12
  273.5 0.7 fusion.23
  274.2 16.3 %fusion.22 = (f32[32,512]{1,0:T(8,128)S(1)}, f32[32,256,512]{2,1,0:T(8,128)S(1)}) fusion(f32[8,32,8,512]{3,2,1,0:T(8,128)} %get-tuple-element.306, s32[]{:T(128)} %get-tuple-element.295, f32[8,32,8,256]{3,2,1,0:T(8,128)} %get-tuple-element.305, f32[32,256]{1,0:T(8,128)S(1)} %dynamic-slice_bitcast_fusion.5), kind=kOutput, calls=%fused_computation.31.clone.1 | convolution fusion | flops 411025408 | bytes 17662976 | tf_op jit(solution)/shard_map/while/body/eval_jaxpr/mkj,mkr->mjr/dot_general | solution.py:12
  291.3 16.3 %fusion.22 = (f32[32,512]{1,0:T(8,128)S(1)}, f32[32,256,512]{2,1,0:T(8,128)S(1)}) fusion(f32[8,32,8,512]{3,2,1,0:T(8,128)} %get-tuple-element.306, s32[]{:T(128)} %get-tuple-element.295, f32[8,32,8,256]{3,2,1,0:T(8,128)} %get-tuple-element.305, f32[32,256]{1,0:T(8,128)S(1)} %dynamic-slice_bitcast_fusion.5), kind=kOutput, calls=%fused_computation.31.clone.1 | convolution fusion | flops 411025408 | bytes 17662976 | tf_op jit(solution)/shard_map/while/body/eval_jaxpr/mkj,mkr->mjr/dot_general | solution.py:12
  308.3 10.0 %all_gather.19 = f32[4,256,128]{2,1,0:T(8,128)S(1)} all-gather(f32[1,256,128]{2,1,0:T(8,128)S(1)} %bitcast.57), channel_id=1, replica_groups=mesh['mkt'=4,'prod'=2,'draw'=4] {'draw'}, dimensions={0}, use_global_device_ids=true | all-gather | bytes 655360 | tf_op jit(solution)/shard_map/all_gather | solution.py:42
  318.3 1.4 multiply_reduce_fusion.1
  319.7 15.3 %all-reduce = (f32[1]{0:T(128)}, f32[1]{0:T(128)}) all-reduce(f32[1]{0:T(128)} %bitcast.15, f32[1]{0:T(128)} %bitcast.14), channel_id=1, replica_groups=mesh['mkt'=4,'prod'=2,'draw'=4] {'mkt','prod'}, use_global_device_ids=true, to_apply=%region_13.14 | all-reduce | flops 2 | bytes 16 | tf_op jit(solution)/shard_map/psum | solution.py:46
  335.0 1.8 fusion.13
  (70 shorter events, 8.6 us)
Async XLA Ops:
  7.2 15.2 %all-gather.2.cloned.1.call-start = ((), (), s32[]{:S(2)}) async-start(), calls=%async_computation | async-start | bytes 3145728 | tf_op jit(solution)/shard_map/all_gather | solution.py:23
  22.4 147.0 %copy-start = (f32[256,128]{1,0:T(8,128)S(1)}, f32[256,128]{1,0:T(8,128)}, u32[]{:S(2)}) copy-start(f32[256,128]{1,0:T(8,128)} %param.9) | copy-start | bytes 393220
  22.4 147.0 %copy-start.1 = (f32[256,128]{1,0:T(8,128)S(1)}, f32[256,128]{1,0:T(8,128)}, u32[]{:S(2)}) copy-start(f32[256,128]{1,0:T(8,128)} %param.10) | copy-start | bytes 393220
Sparse Core Ops, SparseCore 0:
  9.5 12.8 all-gather.1
